TPU v7x, 32 devices: a whole 2x2x4 slice. The times are simulated.
32 devices in a mesh: graph: 8 (over z, y), row: 4 (over x, core).
Axes of the slice: x: 2, y: 2, z: 4, core: 2. Of those that a mesh axis runs over, the one named last changes fastest.
Arguments:
- tiles: bfloat16 [2048, 256, 256], P(('graph', 'row')), parts along dimension 0, may hold values from -0.25 to 0.25
- tile_rows: int32 [2048], P(('graph', 'row')), parts along dimension 0, may hold values from 0 to 15
- tile_cols: int32 [2048], P(('graph', 'row')), parts along dimension 0, may hold values from 0 to 63, as said below
- tile_count: int32 [32], P(('graph', 'row')), parts along dimension 0, may hold values from 8 to 64, as said below
- seeds: float32 [32, 131072], P(None, ('graph', 'row')), parts along dimension 1, may hold values from -6 to 6
- decay: float32 [32], replicated, may hold values from 0.8 to 1
Outputs:
- scores: float32 [32, 131072], P(None, ('graph', 'row')), parts along dimension 1
There are 8 independent parts, one for each index of `graph`. A program takes and returns all parts, laid end to end along the dimension named above; an argument that names none is the same for every part. Nothing has to cross between parts.
Inputs may be any that keep to these rules, and one draw needn't show every extreme that they name: `tile_cols`: among the slots of one row panel, the tile columns that fall in the 16 tile rows of any one panel take at most 4 distinct values; in every draw the live slots of some panel take exactly 4 distinct tile columns of some one panel. Only the first tile_count slots of a panel are live; in every draw one panel has all 64 slots live.
All inputs are finite; a program needn't handle non-finite values.
Results may differ from a plain program's by a relative error of at most 0.0027.
Values may be sent and summed in bfloat16 or wider, within the bound.
A program may use at most 64 MiB of HBM per device.

v0:
```python
import functools

import jax
import jax.numpy as jnp
from jax import lax
from jax.experimental import pallas as pl
from jax.experimental.pallas import tpu as pltpu
from jax.sharding import PartitionSpec as P

TILE = 256
NEED = 4
HALVES = 2
ITERS = 3
MESH = pl.DeviceIdType.MESH
LANES = 128
ROW_PERM, ROW_PLACE, ROW_KEEP, ROW_LAST, ROW_HAS = 0, 1, 2, 3, 4


def fill_tables(rows_ref, cols_ref, count_ref, own_table, wanted_slot, slots, blk, width):
    square = max(LANES, slots)
    lane = lax.broadcasted_iota(jnp.int32, (square, square), 1)
    sub = lax.broadcasted_iota(jnp.int32, (square, square), 0)

    def spread(ref):
        wide = jnp.concatenate(
            [ref[...], jnp.zeros((1, square - slots), jnp.int32)], axis=1
        ) if square > slots else ref[...]
        return jnp.broadcast_to(wide, (square, square))

    live_row = lane < count_ref[0]
    key_row = jnp.where(live_row, spread(rows_ref), blk)
    key_row = jnp.where(lane < slots, key_row, blk + 1)
    col_row = jnp.where(live_row & (lane < slots), spread(cols_ref), -1)
    key_col = jnp.transpose(key_row)[:slots, :]
    col_col = jnp.transpose(col_row)[:slots, :]

    col_t = col_col[:, :1]
    lane_c = lax.broadcasted_iota(jnp.int32, (slots, width), 1)
    hit = (col_t == lane_c).astype(jnp.int32)
    lane_w = lax.broadcasted_iota(jnp.int32, (8, width), 1)
    local = lane_w % blk
    present = jnp.broadcast_to(jnp.max(hit, axis=0, keepdims=True), (8, width))

    def scan(value):
        step = 1
        while step < blk:
            value = value + jnp.where(local >= step, pltpu.roll(value, step, 1), 0)
            step *= 2
        return value

    rank = scan(present) - 1
    which = lax.broadcasted_iota(jnp.int32, (8, width), 0)
    chosen = (present > 0) & (rank == which)
    wanted_slot[...] = scan(jnp.where(chosen, local, 0))

    weight = (lane_w // blk) * NEED + rank
    place_col = jnp.sum(hit * weight[:1, :], axis=1, keepdims=True)
    place_col = jnp.clip(place_col, 0, (width // blk) * NEED - 1)

    key_c = key_col
    key_r = key_row[:slots, :]
    lane_s, sub_s = lane[:slots, :], sub[:slots, :]
    before = (key_r < key_c) | ((key_r == key_c) & (lane_s < sub_s))
    position = jnp.sum((before & (lane_s < slots)).astype(jnp.int32), axis=1, keepdims=True)
    at = position == lane_s
    perm = jnp.sum(jnp.where(at, sub_s, 0), axis=0, keepdims=True)
    place = jnp.sum(jnp.where(at, place_col, 0), axis=0, keepdims=True)
    key_sorted = jnp.sum(jnp.where(at, key_c, 0), axis=0, keepdims=True)
    previous = jnp.sum(jnp.where(position + 1 == lane_s, key_c, 0), axis=0, keepdims=True)
    keep = ((key_sorted == previous) & (lane_s[:1, :] > 0)).astype(jnp.int32)
    last = jnp.sum((key_c <= lane_s).astype(jnp.int32), axis=0, keepdims=True) - 1
    has = jnp.max((key_c == lane_s).astype(jnp.int32), axis=0, keepdims=True)
    own_table[...] = jnp.zeros(own_table.shape, jnp.int32)
    own_table[ROW_PERM:ROW_PERM + 1, :] = perm
    own_table[ROW_PLACE:ROW_PLACE + 1, :] = place
    own_table[ROW_KEEP:ROW_KEEP + 1, :] = keep
    own_table[ROW_LAST:ROW_LAST + 1, :] = jnp.maximum(last, 0)
    own_table[ROW_HAS:ROW_HAS + 1, :] = has


def kernel(
    panels, slots, blk, seed_count, chunks, unroll, halves,
    count_ref, rows_ref, cols_ref, decay_ref, seeds_hbm, tiles_hbm,
    out_ref,
    tiles, turned, seeds_ref, current, outgoing, partial, own_table, wanted, squares,
    own_s, wanted_s,
    tile_sem, seed_sem, table_sem, want_send, want_recv, send_sem, recv_sem, norm_send, norm_recv,
    *arrivals,
):
    me = lax.axis_index("row")
    cores = 2 if panels % 2 == 0 else 1
    chip, core = me // cores, me % cores
    groups = panels // cores
    steps = [(d, e) for d in range(groups - 1, -1, -1) for e in range(cores) if (d, e) != (0, 0)]
    rows = seed_count // halves

    def target(d, e):
        return lax.rem(chip + d, groups) * cores + lax.rem(core + e, cores)

    barrier = pltpu.get_barrier_semaphore()
    for d, e in steps:
        pl.semaphore_signal(
            barrier, inc=1, device_id={"row": target(d, e)}, device_id_type=MESH
        )

    seed_load = pltpu.make_async_copy(seeds_hbm, seeds_ref, seed_sem.at[0])
    seed_load.start()
    per = slots // chunks

    def load(c):
        return pltpu.make_async_copy(
            tiles_hbm.at[pl.ds(c * per, per)], tiles.at[pl.ds(c * per, per)], tile_sem.at[c]
        )

    for c in range(chunks):
        load(c).start()

    fill_tables(rows_ref, cols_ref, count_ref, own_table, wanted, slots, blk, wanted.shape[1])
    pl.semaphore_wait(barrier, panels - 1)

    asks = []
    for n, (d, e) in enumerate(steps):
        ask = pltpu.make_async_remote_copy(
            src_ref=wanted, dst_ref=wanted_s.at[me],
            send_sem=want_send.at[n], recv_sem=want_recv.at[n],
            device_id={"row": target(d, e)}, device_id_type=MESH,
        )
        ask.start()
        asks.append(ask)
    own_copy = pltpu.make_async_copy(own_table, own_s, table_sem.at[0])
    own_copy.start()
    want_copy = pltpu.make_async_copy(wanted, wanted_s.at[me], table_sem.at[1])
    want_copy.start()

    seed_load.wait()
    for h in range(halves):
        for b in range(blk):
            current[h, b] = seeds_ref[
                h * rows:(h + 1) * rows, b * TILE:(b + 1) * TILE
            ].astype(jnp.bfloat16)
    diagonal = lax.broadcasted_iota(jnp.int32, (seed_count, seed_count), 0) == (
        lax.broadcasted_iota(jnp.int32, (seed_count, seed_count), 1)
    )
    decay = jnp.sum(
        jnp.where(diagonal, jnp.broadcast_to(decay_ref[...], diagonal.shape), 0.0),
        axis=1, keepdims=True,
    )

    for ask in asks:
        ask.wait_recv()
    want_copy.wait()

    def exchange(it, h):
        arrived = arrivals[it * halves + h]
        sends = []
        for n, (d, e) in enumerate(steps):
            peer = target(d, e)
            for k in range(NEED):
                outgoing[it, h, n, k] = current[h, wanted_s[peer, k, me * blk + blk - 1]]
            send = pltpu.make_async_remote_copy(
                src_ref=outgoing.at[it, h, n],
                dst_ref=arrived.at[pl.ds(me * NEED, NEED)],
                send_sem=send_sem.at[it, h, n], recv_sem=recv_sem.at[it, h, n],
                device_id={"row": peer}, device_id_type=MESH,
            )
            send.start()
            sends.append(send)
        for k in range(NEED):
            arrived[me * NEED + k] = current[h, wanted_s[me, k, me * blk + blk - 1]]
        return sends

    flying = {(0, h): exchange(0, h) for h in range(halves)}

    def turn(c, carry):
        load(c).wait()
        for i in range(per):
            turned[c * per + i] = jnp.transpose(tiles[c * per + i])
        return carry

    lax.fori_loop(0, chunks, turn, 0)
    own_copy.wait()

    totals = []
    for it in range(ITERS):
        for h in range(halves):
            arrived = arrivals[it * halves + h]
            for send in flying[it, h]:
                send.wait_recv()

            def some(group, acc):
                for u in range(unroll):
                    j = group * unroll + u
                    product = jnp.dot(
                        arrived[own_s[ROW_PLACE, j]], turned[own_s[ROW_PERM, j]],
                        preferred_element_type=jnp.float32,
                    )
                    acc = acc * own_s[ROW_KEEP, j].astype(jnp.float32) + product
                    partial[h, j] = acc
                return acc

            lax.fori_loop(0, slots // unroll, some, jnp.zeros((rows, TILE), jnp.float32))

            mine = slice(h * rows, (h + 1) * rows)
            total = jnp.zeros((rows, TILE), jnp.float32)
            for r in range(blk):
                summed = partial[h, own_s[ROW_LAST, r]] * own_s[ROW_HAS, r].astype(jnp.float32)
                value = decay[mine] * summed + seeds_ref[mine, r * TILE:(r + 1) * TILE]
                if it < ITERS - 1:
                    current[h, r] = value.astype(jnp.bfloat16)
                else:
                    out_ref[mine, r * TILE:(r + 1) * TILE] = value
                    total = total + value * value
            if it < ITERS - 1:
                flying[it + 1, h] = exchange(it + 1, h)
            else:
                totals.append(jnp.sum(total, axis=1, keepdims=True))

    lane = lax.broadcasted_iota(jnp.int32, (8, LANES), 1)
    packed = jnp.zeros((8, LANES), jnp.float32)
    pieces = [t[i:i + 8] for t in totals for i in range(0, rows, 8)]
    for i, piece in enumerate(pieces):
        packed = jnp.where(lane == i, piece, packed)
    squares[me] = packed
    sums = []
    for n, (d, e) in enumerate(steps):
        part = pltpu.make_async_remote_copy(
            src_ref=squares.at[me], dst_ref=squares.at[me],
            send_sem=norm_send.at[n], recv_sem=norm_recv.at[n],
            device_id={"row": target(d, e)}, device_id_type=MESH,
        )
        part.start()
        sums.append(part)
    for sends in flying.values():
        for send in sends:
            send.wait_send()
    for ask in asks:
        ask.wait_send()
    for part in sums:
        part.wait_recv()
    every = squares[0]
    for p in range(1, panels):
        every = every + squares[p]
    scale = 1.0 / jnp.sqrt(every / (panels * blk * TILE) + 1e-06)
    for i in range(len(pieces)):
        one = jnp.sum(jnp.where(lane == i, scale, 0.0), axis=1, keepdims=True)
        out_ref[i * 8:(i + 1) * 8, :] = out_ref[i * 8:(i + 1) * 8, :] * one
    for part in sums:
        part.wait_send()


def per_device(tiles, tile_rows, tile_cols, tile_count, seeds, decay):
    slots = tiles.shape[0]
    seed_count = seeds.shape[0]
    blk = seeds.shape[1] // TILE
    panels = lax.axis_size("row")
    width = -(-panels * blk // LANES) * LANES
    square = max(LANES, slots)
    chunks = 8 if slots % 8 == 0 else 1
    unroll = 64 if slots % 64 == 0 else 1
    halves = HALVES if seed_count % (16 * HALVES) == 0 else 1
    rows = seed_count // halves
    peers = panels - 1
    vmem = pl.BlockSpec(memory_space=pltpu.VMEM)
    anywhere = pl.BlockSpec(memory_space=pl.ANY)
    dma = pltpu.SemaphoreType.DMA
    return pl.pallas_call(
        functools.partial(kernel, panels, slots, blk, seed_count, chunks, unroll, halves),
        out_shape=jax.ShapeDtypeStruct(seeds.shape, jnp.float32),
        in_specs=[
            pl.BlockSpec(memory_space=pltpu.SMEM), vmem, vmem, vmem, anywhere, anywhere,
        ],
        out_specs=vmem,
        scratch_shapes=[
            pltpu.VMEM((slots, TILE, TILE), jnp.bfloat16),
            pltpu.VMEM((slots, TILE, TILE), jnp.bfloat16),
            pltpu.VMEM(seeds.shape, jnp.float32),
            pltpu.VMEM((halves, blk, rows, TILE), jnp.bfloat16),
            pltpu.VMEM((ITERS, halves, peers, NEED, rows, TILE), jnp.bfloat16),
            pltpu.VMEM((halves, slots, rows, TILE), jnp.float32),
            pltpu.VMEM((8, square), jnp.int32),
            pltpu.VMEM((8, width), jnp.int32),
            pltpu.VMEM((panels, 8, LANES), jnp.float32),
            pltpu.SMEM((8, square), jnp.int32),
            pltpu.SMEM((panels, 8, width), jnp.int32),
            dma((chunks,)), dma((1,)), dma((2,)), dma((peers,)), dma((peers,)),
            dma((ITERS, halves, peers)), dma((ITERS, halves, peers)),
            dma((peers,)), dma((peers,)),
            *[
                pltpu.VMEM((panels * NEED, rows, TILE), jnp.bfloat16)
                for _ in range(ITERS * halves)
            ],
        ],
        compiler_params=pltpu.CompilerParams(
            collective_id=0, has_side_effects=True, vmem_limit_bytes=53 * 2**20
        ),
    )(
        tile_count, tile_rows.reshape(1, slots), tile_cols.reshape(1, slots),
        decay.reshape(1, seed_count), seeds, tiles,
    )


def solution(mesh):
    in_specs = (
        P(("graph", "row"), None, None),
        P(("graph", "row")),
        P(("graph", "row")),
        P(("graph", "row")),
        P(None, ("graph", "row")),
        P(),
    )
    out_specs = P(None, ("graph", "row"))
    return jax.shard_map(
        per_device, mesh=mesh, in_specs=in_specs, out_specs=out_specs, check_vma=False
    )
```

profile of v0, /device:TPU:0, one launch (start us, length us, event | category | flops | bytes accessed | tf_op | source)
XLA Modules:
  0.0 27.7 jit_solution(90084906953495617)
XLA Ops:
  0.7 0.0 copy-start
  0.7 0.6 %copy-done = s32[64]{0:T(128)S(1)} copy-done((s32[64]{0:T(128)S(1)}, s32[64]{0:T(128)}, u32[]{:S(2)}) %copy-start) | copy-done | bytes 280
  1.3 0.0 copy-start.1
  1.3 0.7 %copy-done.1 = s32[64]{0:T(128)S(1)} copy-done((s32[64]{0:T(128)S(1)}, s32[64]{0:T(128)}, u32[]{:S(2)}) %copy-start.1) | copy-done | bytes 280
  2.0 0.0 copy-start.2
  2.0 0.7 %copy-done.2 = f32[32]{0:T(128)S(1)} copy-done((f32[32]{0:T(128)S(1)}, f32[32]{0:T(128)}, u32[]{:S(2)}) %copy-start.2) | copy-done | bytes 152
  2.6 24.3 %shard_map.64 = f32[32,4096]{1,0:T(8,128)S(1)} custom-call(s32[1]{0:T(128)S(6)} %copy.8.count_ref, s32[1,64]{1,0:T(1,128)S(1)} %bitcast.3, s32[1,64]{1,0:T(1,128)S(1)} %bitcast.4, f32[1,32]{1,0:T(1,128)S(1)} %bitcast.5, f32[32,4096]{1,0:T(8,128)} %seeds_hbm.1, bf16[64,256,256]{2,1,0:T(8,128)(2,1)} %tiles_hbm.1), custom_call_target="tpu_custom_call" | custom-call | tf_op jit(solution)/shard_map/pallas_call | solution.py:266
  27.0 0.8 %copy.9 = f32[32,4096]{1,0:T(8,128)} copy(f32[32,4096]{1,0:T(8,128)S(1)} %shard_map.64) | data formatting | bytes 1048576
Async XLA Ops:
  0.7 0.7 %copy-start = (s32[64]{0:T(128)S(1)}, s32[64]{0:T(128)}, u32[]{:S(2)}) copy-start(s32[64]{0:T(128)} %param.7) | copy-start | bytes 772
  1.3 0.7 %copy-start.1 = (s32[64]{0:T(128)S(1)}, s32[64]{0:T(128)}, u32[]{:S(2)}) copy-start(s32[64]{0:T(128)} %param.8) | copy-start | bytes 772
  2.0 0.7 %copy-start.2 = (f32[32]{0:T(128)S(1)}, f32[32]{0:T(128)}, u32[]{:S(2)}) copy-start(f32[32]{0:T(128)} %param.11) | copy-start | bytes 388
where the time goes:
time: 27.9 us; the launch traced here: 27.7 us
  Pallas kernels  24.3 us (87%)
  local copies, waits for them, and re-layouts  2.75 us (10%)
  between operations  0.67 us (2%)
    pallas_call x1, Pallas kernels, per_device(): pl.pallas_call(functools.partial(kernel, panels, slots, blk, seed_count,...  24.3 us
    unnamed x7, local copies, waits for them, and re-layouts  2.75 us

commit v1 on v0

--- a/solution.py
+++ b/solution.py
@@ -16,25 +16,19 @@
 ROW_PERM, ROW_PLACE, ROW_KEEP, ROW_LAST, ROW_HAS = 0, 1, 2, 3, 4
 
 
-def fill_tables(rows_ref, cols_ref, count_ref, own_table, wanted_slot, slots, blk, width):
+def spread(ref, slots, square):
+    wide = jnp.concatenate(
+        [ref[...], jnp.zeros((1, square - slots), jnp.int32)], axis=1
+    ) if square > slots else ref[...]
+    return jnp.broadcast_to(wide, (square, square))
+
+
+def fill_wanted(cols_ref, count, wanted, slots, blk):
+    width = wanted.shape[1]
     square = max(LANES, slots)
     lane = lax.broadcasted_iota(jnp.int32, (square, square), 1)
-    sub = lax.broadcasted_iota(jnp.int32, (square, square), 0)
-
-    def spread(ref):
-        wide = jnp.concatenate(
-            [ref[...], jnp.zeros((1, square - slots), jnp.int32)], axis=1
-        ) if square > slots else ref[...]
-        return jnp.broadcast_to(wide, (square, square))
-
-    live_row = lane < count_ref[0]
-    key_row = jnp.where(live_row, spread(rows_ref), blk)
-    key_row = jnp.where(lane < slots, key_row, blk + 1)
-    col_row = jnp.where(live_row & (lane < slots), spread(cols_ref), -1)
-    key_col = jnp.transpose(key_row)[:slots, :]
-    col_col = jnp.transpose(col_row)[:slots, :]
-
-    col_t = col_col[:, :1]
+    col_row = jnp.where((lane < count) & (lane < slots), spread(cols_ref, slots, square), -1)
+    col_t = jnp.transpose(col_row)[:slots, :1]
     lane_c = lax.broadcasted_iota(jnp.int32, (slots, width), 1)
     hit = (col_t == lane_c).astype(jnp.int32)
     lane_w = lax.broadcasted_iota(jnp.int32, (8, width), 1)
@@ -51,14 +45,22 @@
     rank = scan(present) - 1
     which = lax.broadcasted_iota(jnp.int32, (8, width), 0)
     chosen = (present > 0) & (rank == which)
-    wanted_slot[...] = scan(jnp.where(chosen, local, 0))
-
+    wanted[...] = scan(jnp.where(chosen, local, 0))
     weight = (lane_w // blk) * NEED + rank
+    return hit, weight
+
+
+def fill_own(rows_ref, count, own_table, hit, weight, slots, blk):
+    width = hit.shape[1]
+    square = max(LANES, slots)
+    lane = lax.broadcasted_iota(jnp.int32, (square, square), 1)
+    sub = lax.broadcasted_iota(jnp.int32, (square, square), 0)
+    key_row = jnp.where(lane < count, spread(rows_ref, slots, square), blk)
+    key_row = jnp.where(lane < slots, key_row, blk + 1)
+    key_c = jnp.transpose(key_row)[:slots, :]
+    key_r = key_row[:slots, :]
     place_col = jnp.sum(hit * weight[:1, :], axis=1, keepdims=True)
     place_col = jnp.clip(place_col, 0, (width // blk) * NEED - 1)
-
-    key_c = key_col
-    key_r = key_row[:slots, :]
     lane_s, sub_s = lane[:slots, :], sub[:slots, :]
     before = (key_r < key_c) | ((key_r == key_c) & (lane_s < sub_s))
     position = jnp.sum((before & (lane_s < slots)).astype(jnp.int32), axis=1, keepdims=True)
@@ -80,28 +82,35 @@
 
 def kernel(
     panels, slots, blk, seed_count, chunks, unroll, halves,
-    count_ref, rows_ref, cols_ref, decay_ref, seeds_hbm, tiles_hbm,
+    count_ref, cols_hbm, rows_hbm, decay_hbm, seeds_hbm, tiles_hbm,
     out_ref,
     tiles, turned, seeds_ref, current, outgoing, partial, own_table, wanted, squares,
-    own_s, wanted_s,
-    tile_sem, seed_sem, table_sem, want_send, want_recv, send_sem, recv_sem, norm_send, norm_recv,
+    rows_ref, cols_ref, decay_ref, own_s, wanted_s,
+    tile_sem, seed_sem, small_sem, table_sem,
+    want_send, want_recv, send_sem, recv_sem, norm_send, norm_recv,
     *arrivals,
 ):
     me = lax.axis_index("row")
     cores = 2 if panels % 2 == 0 else 1
     chip, core = me // cores, me % cores
     groups = panels // cores
-    steps = [(d, e) for d in range(groups - 1, -1, -1) for e in range(cores) if (d, e) != (0, 0)]
     rows = seed_count // halves
-
-    def target(d, e):
-        return lax.rem(chip + d, groups) * cores + lax.rem(core + e, cores)
-
+    peers = [
+        lax.rem(chip + d, groups) * cores + e
+        for d in range(groups - 1, 0, -1) for e in range(cores)
+    ] + [chip * cores + lax.rem(core + e, cores) for e in range(1, cores)]
+
+    small = [
+        pltpu.make_async_copy(src, dst, small_sem.at[n])
+        for n, (src, dst) in enumerate([
+            (cols_hbm, cols_ref), (rows_hbm, rows_ref), (decay_hbm, decay_ref),
+        ])
+    ]
+    for copy in small:
+        copy.start()
     barrier = pltpu.get_barrier_semaphore()
-    for d, e in steps:
-        pl.semaphore_signal(
-            barrier, inc=1, device_id={"row": target(d, e)}, device_id_type=MESH
-        )
+    for peer in peers:
+        pl.semaphore_signal(barrier, inc=1, device_id={"row": peer}, device_id_type=MESH)
 
     seed_load = pltpu.make_async_copy(seeds_hbm, seeds_ref, seed_sem.at[0])
     seed_load.start()
@@ -115,22 +124,27 @@
     for c in range(chunks):
         load(c).start()
 
-    fill_tables(rows_ref, cols_ref, count_ref, own_table, wanted, slots, blk, wanted.shape[1])
+    small[0].wait()
+    count = count_ref[0]
+    hit, weight = fill_wanted(cols_ref, count, wanted, slots, blk)
     pl.semaphore_wait(barrier, panels - 1)
 
-    asks = []
-    for n, (d, e) in enumerate(steps):
-        ask = pltpu.make_async_remote_copy(
-            src_ref=wanted, dst_ref=wanted_s.at[me],
-            send_sem=want_send.at[n], recv_sem=want_recv.at[n],
-            device_id={"row": target(d, e)}, device_id_type=MESH,
-        )
-        ask.start()
-        asks.append(ask)
+    def ask(n, peer, source):
+        return pltpu.make_async_remote_copy(
+            src_ref=wanted, dst_ref=wanted_s.at[source],
+            send_sem=want_send.at[n], recv_sem=want_recv.at[source],
+            device_id={"row": peer}, device_id_type=MESH,
+        )
+
+    for n, peer in enumerate(peers):
+        ask(n, peer, me).start()
+    want_copy = pltpu.make_async_copy(wanted, wanted_s.at[me], table_sem.at[1])
+    want_copy.start()
+    small[1].wait()
+    fill_own(rows_ref, count, own_table, hit, weight, slots, blk)
     own_copy = pltpu.make_async_copy(own_table, own_s, table_sem.at[0])
     own_copy.start()
-    want_copy = pltpu.make_async_copy(wanted, wanted_s.at[me], table_sem.at[1])
-    want_copy.start()
+    small[2].wait()
 
     seed_load.wait()
     for h in range(halves):
@@ -146,30 +160,29 @@
         axis=1, keepdims=True,
     )
 
-    for ask in asks:
-        ask.wait_recv()
+    for n, peer in enumerate(peers):
+        ask(n, peer, peer).wait_recv()
     want_copy.wait()
+
+    def ship(it, h, n, peer, source):
+        return pltpu.make_async_remote_copy(
+            src_ref=outgoing.at[it, h, n],
+            dst_ref=arrivals[it * halves + h].at[pl.ds(source * NEED, NEED)],
+            send_sem=send_sem.at[it, h, n], recv_sem=recv_sem.at[it, h, source],
+            device_id={"row": peer}, device_id_type=MESH,
+        )
 
     def exchange(it, h):
         arrived = arrivals[it * halves + h]
-        sends = []
-        for n, (d, e) in enumerate(steps):
-            peer = target(d, e)
+        for n, peer in enumerate(peers):
             for k in range(NEED):
                 outgoing[it, h, n, k] = current[h, wanted_s[peer, k, me * blk + blk - 1]]
-            send = pltpu.make_async_remote_copy(
-                src_ref=outgoing.at[it, h, n],
-                dst_ref=arrived.at[pl.ds(me * NEED, NEED)],
-                send_sem=send_sem.at[it, h, n], recv_sem=recv_sem.at[it, h, n],
-                device_id={"row": peer}, device_id_type=MESH,
-            )
-            send.start()
-            sends.append(send)
+            ship(it, h, n, peer, me).start()
         for k in range(NEED):
             arrived[me * NEED + k] = current[h, wanted_s[me, k, me * blk + blk - 1]]
-        return sends
-
-    flying = {(0, h): exchange(0, h) for h in range(halves)}
+
+    for h in range(halves):
+        exchange(0, h)
 
     def turn(c, carry):
         load(c).wait()
@@ -184,8 +197,8 @@
     for it in range(ITERS):
         for h in range(halves):
             arrived = arrivals[it * halves + h]
-            for send in flying[it, h]:
-                send.wait_recv()
+            for n, peer in enumerate(peers):
+                ship(it, h, n, peer, peer).wait_recv()
 
             def some(group, acc):
                 for u in range(unroll):
@@ -211,7 +224,7 @@
                     out_ref[mine, r * TILE:(r + 1) * TILE] = value
                     total = total + value * value
             if it < ITERS - 1:
-                flying[it + 1, h] = exchange(it + 1, h)
+                exchange(it + 1, h)
             else:
                 totals.append(jnp.sum(total, axis=1, keepdims=True))
 
@@ -221,22 +234,23 @@
     for i, piece in enumerate(pieces):
         packed = jnp.where(lane == i, piece, packed)
     squares[me] = packed
-    sums = []
-    for n, (d, e) in enumerate(steps):
-        part = pltpu.make_async_remote_copy(
-            src_ref=squares.at[me], dst_ref=squares.at[me],
-            send_sem=norm_send.at[n], recv_sem=norm_recv.at[n],
-            device_id={"row": target(d, e)}, device_id_type=MESH,
-        )
-        part.start()
-        sums.append(part)
-    for sends in flying.values():
-        for send in sends:
-            send.wait_send()
-    for ask in asks:
-        ask.wait_send()
-    for part in sums:
-        part.wait_recv()
+
+    def share(n, peer, source):
+        return pltpu.make_async_remote_copy(
+            src_ref=squares.at[me], dst_ref=squares.at[source],
+            send_sem=norm_send.at[n], recv_sem=norm_recv.at[source],
+            device_id={"row": peer}, device_id_type=MESH,
+        )
+
+    for n, peer in enumerate(peers):
+        share(n, peer, me).start()
+    for n, peer in enumerate(peers):
+        for it in range(ITERS):
+            for h in range(halves):
+                ship(it, h, n, peer, me).wait_send()
+        ask(n, peer, me).wait_send()
+    for n, peer in enumerate(peers):
+        share(n, peer, peer).wait_recv()
     every = squares[0]
     for p in range(1, panels):
         every = every + squares[p]
@@ -244,8 +258,8 @@
     for i in range(len(pieces)):
         one = jnp.sum(jnp.where(lane == i, scale, 0.0), axis=1, keepdims=True)
         out_ref[i * 8:(i + 1) * 8, :] = out_ref[i * 8:(i + 1) * 8, :] * one
-    for part in sums:
-        part.wait_send()
+    for n, peer in enumerate(peers):
+        share(n, peer, me).wait_send()
 
 
 def per_device(tiles, tile_rows, tile_cols, tile_count, seeds, decay):
@@ -261,14 +275,11 @@
     rows = seed_count // halves
     peers = panels - 1
     vmem = pl.BlockSpec(memory_space=pltpu.VMEM)
-    anywhere = pl.BlockSpec(memory_space=pl.ANY)
     dma = pltpu.SemaphoreType.DMA
     return pl.pallas_call(
         functools.partial(kernel, panels, slots, blk, seed_count, chunks, unroll, halves),
         out_shape=jax.ShapeDtypeStruct(seeds.shape, jnp.float32),
-        in_specs=[
-            pl.BlockSpec(memory_space=pltpu.SMEM), vmem, vmem, vmem, anywhere, anywhere,
-        ],
+        in_specs=[pl.BlockSpec(memory_space=pltpu.SMEM)] + [pl.BlockSpec(memory_space=pltpu.HBM)] * 5,
         out_specs=vmem,
         scratch_shapes=[
             pltpu.VMEM((slots, TILE, TILE), jnp.bfloat16),
@@ -280,11 +291,14 @@
             pltpu.VMEM((8, square), jnp.int32),
             pltpu.VMEM((8, width), jnp.int32),
             pltpu.VMEM((panels, 8, LANES), jnp.float32),
+            pltpu.VMEM((1, slots), jnp.int32),
+            pltpu.VMEM((1, slots), jnp.int32),
+            pltpu.VMEM((1, seed_count), jnp.float32),
             pltpu.SMEM((8, square), jnp.int32),
             pltpu.SMEM((panels, 8, width), jnp.int32),
-            dma((chunks,)), dma((1,)), dma((2,)), dma((peers,)), dma((peers,)),
-            dma((ITERS, halves, peers)), dma((ITERS, halves, peers)),
-            dma((peers,)), dma((peers,)),
+            dma((chunks,)), dma((1,)), dma((3,)), dma((2,)), dma((peers,)), dma((panels,)),
+            dma((ITERS, halves, peers)), dma((ITERS, halves, panels)),
+            dma((peers,)), dma((panels,)),
             *[
                 pltpu.VMEM((panels * NEED, rows, TILE), jnp.bfloat16)
                 for _ in range(ITERS * halves)
@@ -293,10 +307,13 @@
         compiler_params=pltpu.CompilerParams(
             collective_id=0, has_side_effects=True, vmem_limit_bytes=53 * 2**20
         ),
-    )(
-        tile_count, tile_rows.reshape(1, slots), tile_cols.reshape(1, slots),
-        decay.reshape(1, seed_count), seeds, tiles,
-    )
+    )(tile_count, *[
+        pltpu.with_memory_space_constraint(one, pltpu.HBM)
+        for one in (
+            tile_cols.reshape(1, slots), tile_rows.reshape(1, slots),
+            decay.reshape(1, seed_count), seeds, tiles,
+        )
+    ])
 
 
 def solution(mesh):

time: 27.9 us -> 26.3 us (0.943)
  local copies, waits for them, and re-layouts: 2.75 us -> 0.8 us
  Pallas kernels: 24.3 us -> 24.7 us
    unnamed x7 -> x1, local copies, waits for them, and re-layouts: 2.75 us -> 0.8 us
    pallas_call x1, Pallas kernels: 24.3 us -> 24.7 us  [per_device(): pl.pallas_call(functools.partial(kernel, panels, slots, blk, seed_count,...]
where the time goes in v1:
time: 26.3 us; the launch traced here: 26.2 us
  Pallas kernels  24.7 us (94%)
  local copies, waits for them, and re-layouts  0.8 us (3%)
  between operations  0.66 us (3%)
    pallas_call x1, Pallas kernels, per_device(): pl.pallas_call(functools.partial(kernel, panels, slots, blk, seed_count,...  24.7 us
    unnamed x1, local copies, waits for them, and re-layouts  0.8 us

profile of v1, /device:TPU:0, one launch (start us, length us, event | category | flops | bytes accessed | tf_op | source)
XLA Modules:
  0.0 26.2 jit_solution(112353088751519367)
XLA Ops:
  0.7 24.7 %shard_map.64 = f32[32,4096]{1,0:T(8,128)S(1)} custom-call(s32[1]{0:T(128)S(6)} %copy.8.count_ref, s32[1,64]{1,0:T(1,128)} %bitcast.3, s32[1,64]{1,0:T(1,128)} %bitcast.4, f32[1,32]{1,0:T(1,128)} %bitcast.5, f32[32,4096]{1,0:T(8,128)} %seeds_hbm.1, bf16[64,256,256]{2,1,0:T(8,128)(2,1)} %tiles_hbm.1), custom_call_target="tpu_custom_call" | custom-call | tf_op jit(solution)/shard_map/pallas_call | solution.py:279
  25.4 0.8 %copy.9 = f32[32,4096]{1,0:T(8,128)} copy(f32[32,4096]{1,0:T(8,128)S(1)} %shard_map.64) | data formatting | bytes 1048576

commit v2 on v1

--- a/solution.py
+++ b/solution.py
@@ -10,10 +10,11 @@
 TILE = 256
 NEED = 4
 HALVES = 2
+PARTS = 2
 ITERS = 3
 MESH = pl.DeviceIdType.MESH
 LANES = 128
-ROW_PERM, ROW_PLACE, ROW_KEEP, ROW_LAST, ROW_HAS = 0, 1, 2, 3, 4
+ROW_PERM, ROW_PLACE, ROW_KEEP, ROW_LAST, ROW_HAS, ROW_COL = 0, 1, 2, 3, 4, 5
 
 
 def spread(ref, slots, square):
@@ -47,10 +48,10 @@
     chosen = (present > 0) & (rank == which)
     wanted[...] = scan(jnp.where(chosen, local, 0))
     weight = (lane_w // blk) * NEED + rank
-    return hit, weight
-
-
-def fill_own(rows_ref, count, own_table, hit, weight, slots, blk):
+    return hit, weight, col_t
+
+
+def fill_own(rows_ref, count, own_table, hit, weight, col_t, slots, blk):
     width = hit.shape[1]
     square = max(LANES, slots)
     lane = lax.broadcasted_iota(jnp.int32, (square, square), 1)
@@ -67,6 +68,7 @@
     at = position == lane_s
     perm = jnp.sum(jnp.where(at, sub_s, 0), axis=0, keepdims=True)
     place = jnp.sum(jnp.where(at, place_col, 0), axis=0, keepdims=True)
+    column = jnp.sum(jnp.where(at, jnp.clip(col_t, 0, width - 1), 0), axis=0, keepdims=True)
     key_sorted = jnp.sum(jnp.where(at, key_c, 0), axis=0, keepdims=True)
     previous = jnp.sum(jnp.where(position + 1 == lane_s, key_c, 0), axis=0, keepdims=True)
     keep = ((key_sorted == previous) & (lane_s[:1, :] > 0)).astype(jnp.int32)
@@ -78,6 +80,7 @@
     own_table[ROW_KEEP:ROW_KEEP + 1, :] = keep
     own_table[ROW_LAST:ROW_LAST + 1, :] = jnp.maximum(last, 0)
     own_table[ROW_HAS:ROW_HAS + 1, :] = has
+    own_table[ROW_COL:ROW_COL + 1, :] = column
 
 
 def kernel(
@@ -88,6 +91,7 @@
     rows_ref, cols_ref, decay_ref, own_s, wanted_s,
     tile_sem, seed_sem, small_sem, table_sem,
     want_send, want_recv, send_sem, recv_sem, norm_send, norm_recv,
+    bulk_send, bulk_recv, pass_send, pass_recv, near_send, near_recv, whole,
     *arrivals,
 ):
     me = lax.axis_index("row")
@@ -122,11 +126,15 @@
         )
 
     for c in range(chunks):
-        load(c).start()
+        load(c).start(priority=1)
 
     small[0].wait()
     count = count_ref[0]
-    hit, weight = fill_wanted(cols_ref, count, wanted, slots, blk)
+    hit, weight, col_t = fill_wanted(cols_ref, count, wanted, slots, blk)
+    seed_load.wait()
+    for b in range(blk):
+        nodes = slice(b * TILE, (b + 1) * TILE)
+        whole[me * blk + b] = seeds_ref[:rows, nodes].astype(jnp.bfloat16)
     pl.semaphore_wait(barrier, panels - 1)
 
     def ask(n, peer, source):
@@ -138,16 +146,50 @@
 
     for n, peer in enumerate(peers):
         ask(n, peer, me).start()
+    span = blk // PARTS
+    partner = chip * cores + (cores - 1 - core)
+
+    def block(source, part):
+        return whole.at[pl.ds(source * blk + part * span, span)]
+
+    def bulk(d, part, source):
+        far = lax.rem(chip + d, groups) * cores + (cores - 1 - core)
+        return pltpu.make_async_remote_copy(
+            src_ref=block(source, part), dst_ref=block(source, part),
+            send_sem=bulk_send.at[d - 1, part], recv_sem=bulk_recv.at[d - 1, part],
+            device_id={"row": far}, device_id_type=MESH,
+        )
+
+    def hand(d, part, source):
+        return pltpu.make_async_remote_copy(
+            src_ref=block(source, part), dst_ref=block(source, part),
+            send_sem=pass_send.at[d - 1, part], recv_sem=pass_recv.at[d - 1, part],
+            device_id={"row": partner}, device_id_type=MESH,
+        )
+
+    def near(source):
+        return pltpu.make_async_remote_copy(
+            src_ref=whole.at[pl.ds(source * blk, blk)], dst_ref=whole.at[pl.ds(source * blk, blk)],
+            send_sem=near_send.at[0], recv_sem=near_recv.at[0],
+            device_id={"row": partner}, device_id_type=MESH,
+        )
+
+    def origin(d, index):
+        return lax.rem(chip + groups - d, groups) * cores + index
+
+    for part in range(PARTS):
+        for d in range(1, groups):
+            bulk(d, part, me).start()
+    if cores > 1:
+        near(me).start()
     want_copy = pltpu.make_async_copy(wanted, wanted_s.at[me], table_sem.at[1])
     want_copy.start()
     small[1].wait()
-    fill_own(rows_ref, count, own_table, hit, weight, slots, blk)
+    fill_own(rows_ref, count, own_table, hit, weight, col_t, slots, blk)
     own_copy = pltpu.make_async_copy(own_table, own_s, table_sem.at[0])
     own_copy.start()
     small[2].wait()
-
-    seed_load.wait()
-    for h in range(halves):
+    for h in range(1, halves):
         for b in range(blk):
             current[h, b] = seeds_ref[
                 h * rows:(h + 1) * rows, b * TILE:(b + 1) * TILE
@@ -160,6 +202,13 @@
         axis=1, keepdims=True,
     )
 
+    def turn(c, carry):
+        load(c).wait()
+        for i in range(per):
+            turned[c * per + i] = jnp.transpose(tiles[c * per + i])
+        return carry
+
+    lax.fori_loop(0, chunks, turn, 0)
     for n, peer in enumerate(peers):
         ask(n, peer, peer).wait_recv()
     want_copy.wait()
@@ -181,30 +230,37 @@
         for k in range(NEED):
             arrived[me * NEED + k] = current[h, wanted_s[me, k, me * blk + blk - 1]]
 
-    for h in range(halves):
+    for h in range(1, halves):
         exchange(0, h)
-
-    def turn(c, carry):
-        load(c).wait()
-        for i in range(per):
-            turned[c * per + i] = jnp.transpose(tiles[c * per + i])
-        return carry
-
-    lax.fori_loop(0, chunks, turn, 0)
+    for part in range(PARTS):
+        for d in range(1, groups):
+            source = origin(d, cores - 1 - core)
+            bulk(d, part, source).wait_recv()
+            if cores > 1:
+                hand(d, part, source).start()
+
     own_copy.wait()
 
     totals = []
     for it in range(ITERS):
         for h in range(halves):
-            arrived = arrivals[it * halves + h]
-            for n, peer in enumerate(peers):
-                ship(it, h, n, peer, peer).wait_recv()
+            first = it == 0 and h == 0
+            arrived = whole if first else arrivals[it * halves + h]
+            row_at = ROW_COL if first else ROW_PLACE
+            if first and cores > 1:
+                near(partner).wait_recv()
+                for part in range(PARTS):
+                    for d in range(1, groups):
+                        hand(d, part, origin(d, core)).wait_recv()
+            if not first:
+                for n, peer in enumerate(peers):
+                    ship(it, h, n, peer, peer).wait_recv()
 
             def some(group, acc):
                 for u in range(unroll):
                     j = group * unroll + u
                     product = jnp.dot(
-                        arrived[own_s[ROW_PLACE, j]], turned[own_s[ROW_PERM, j]],
+                        arrived[own_s[row_at, j]], turned[own_s[ROW_PERM, j]],
                         preferred_element_type=jnp.float32,
                     )
                     acc = acc * own_s[ROW_KEEP, j].astype(jnp.float32) + product
@@ -247,8 +303,16 @@
     for n, peer in enumerate(peers):
         for it in range(ITERS):
             for h in range(halves):
-                ship(it, h, n, peer, me).wait_send()
+                if (it, h) != (0, 0):
+                    ship(it, h, n, peer, me).wait_send()
         ask(n, peer, me).wait_send()
+    for part in range(PARTS):
+        for d in range(1, groups):
+            bulk(d, part, me).wait_send()
+            if cores > 1:
+                hand(d, part, origin(d, cores - 1 - core)).wait_send()
+    if cores > 1:
+        near(me).wait_send()
     for n, peer in enumerate(peers):
         share(n, peer, peer).wait_recv()
     every = squares[0]
@@ -274,6 +338,7 @@
     halves = HALVES if seed_count % (16 * HALVES) == 0 else 1
     rows = seed_count // halves
     peers = panels - 1
+    far = max(panels // (2 if panels % 2 == 0 else 1) - 1, 1)
     vmem = pl.BlockSpec(memory_space=pltpu.VMEM)
     dma = pltpu.SemaphoreType.DMA
     return pl.pallas_call(
@@ -299,6 +364,9 @@
             dma((chunks,)), dma((1,)), dma((3,)), dma((2,)), dma((peers,)), dma((panels,)),
             dma((ITERS, halves, peers)), dma((ITERS, halves, panels)),
             dma((peers,)), dma((panels,)),
+            dma((far, PARTS)), dma((far, PARTS)), dma((far, PARTS)), dma((far, PARTS)),
+            dma((1,)), dma((1,)),
+            pltpu.VMEM((panels * blk, rows, TILE), jnp.bfloat16),
             *[
                 pltpu.VMEM((panels * NEED, rows, TILE), jnp.bfloat16)
                 for _ in range(ITERS * halves)

time: 26.3 us -> 25.3 us (0.962)
  Pallas kernels: 24.7 us -> 23.7 us
    pallas_call x1, Pallas kernels: 24.7 us -> 23.7 us  [per_device(): pl.pallas_call(functools.partial(kernel, panels, slots, blk, seed_count,...]
where the time goes in v2:
time: 25.3 us; the launch traced here: 25.1 us
  Pallas kernels  23.7 us (94%)
  local copies, waits for them, and re-layouts  0.8 us (3%)
  between operations  0.66 us (3%)
    pallas_call x1, Pallas kernels, per_device(): pl.pallas_call(functools.partial(kernel, panels, slots, blk, seed_count,...  23.7 us
    unnamed x1, local copies, waits for them, and re-layouts  0.8 us

profile of v2, /device:TPU:0, one launch (start us, length us, event | category | flops | bytes accessed | tf_op | source)
XLA Modules:
  0.0 25.1 jit_solution(10922649921559089032)
XLA Ops:
  0.7 23.7 %shard_map.64 = f32[32,4096]{1,0:T(8,128)S(1)} custom-call(s32[1]{0:T(128)S(6)} %copy.8.count_ref, s32[1,64]{1,0:T(1,128)} %bitcast.3, s32[1,64]{1,0:T(1,128)} %bitcast.4, f32[1,32]{1,0:T(1,128)} %bitcast.5, f32[32,4096]{1,0:T(8,128)} %seeds_hbm.1, bf16[64,256,256]{2,1,0:T(8,128)(2,1)} %tiles_hbm.1), custom_call_target="tpu_custom_call" | custom-call | tf_op jit(solution)/shard_map/pallas_call | solution.py:344
  24.3 0.8 %copy.9 = f32[32,4096]{1,0:T(8,128)} copy(f32[32,4096]{1,0:T(8,128)S(1)} %shard_map.64) | data formatting | bytes 1048576

commit v3 on v2

--- a/solution.py
+++ b/solution.py
@@ -89,10 +89,33 @@
     out_ref,
     tiles, turned, seeds_ref, current, outgoing, partial, own_table, wanted, squares,
     rows_ref, cols_ref, decay_ref, own_s, wanted_s,
+    whole, *arrivals,
+):
+    dma = pltpu.SemaphoreType.DMA
+    peers, far = panels - 1, max(panels // (2 if panels % 2 == 0 else 1) - 1, 1)
+    pl.run_scoped(
+        functools.partial(
+            body, panels, slots, blk, seed_count, chunks, unroll, halves,
+            count_ref, cols_hbm, rows_hbm, decay_hbm, seeds_hbm, tiles_hbm,
+            out_ref,
+            tiles, turned, seeds_ref, current, outgoing, partial, own_table, wanted, squares,
+            rows_ref, cols_ref, decay_ref, own_s, wanted_s, whole, arrivals,
+        ),
+        dma((chunks,)), dma((halves,)), dma((3,)), dma((2,)), dma((peers,)), dma((panels,)),
+        dma((ITERS, halves, peers)), dma((ITERS, halves, panels)), dma((peers,)), dma((panels,)),
+        dma((far, PARTS)), dma((far, PARTS)), dma((far, PARTS)), dma((far, PARTS)), dma((1,)), dma((1,)),
+    )
+
+
+def body(
+    panels, slots, blk, seed_count, chunks, unroll, halves,
+    count_ref, cols_hbm, rows_hbm, decay_hbm, seeds_hbm, tiles_hbm,
+    out_ref,
+    tiles, turned, seeds_ref, current, outgoing, partial, own_table, wanted, squares,
+    rows_ref, cols_ref, decay_ref, own_s, wanted_s, whole, arrivals,
     tile_sem, seed_sem, small_sem, table_sem,
     want_send, want_recv, send_sem, recv_sem, norm_send, norm_recv,
-    bulk_send, bulk_recv, pass_send, pass_recv, near_send, near_recv, whole,
-    *arrivals,
+    bulk_send, bulk_recv, pass_send, pass_recv, near_send, near_recv,
 ):
     me = lax.axis_index("row")
     cores = 2 if panels % 2 == 0 else 1
@@ -116,8 +139,12 @@
     for peer in peers:
         pl.semaphore_signal(barrier, inc=1, device_id={"row": peer}, device_id_type=MESH)
 
-    seed_load = pltpu.make_async_copy(seeds_hbm, seeds_ref, seed_sem.at[0])
-    seed_load.start()
+    def seed_load(h):
+        mine = pl.ds(h * rows, rows)
+        return pltpu.make_async_copy(seeds_hbm.at[mine], seeds_ref.at[mine], seed_sem.at[h])
+
+    for h in range(halves):
+        seed_load(h).start()
     per = slots // chunks
 
     def load(c):
@@ -131,7 +158,7 @@
     small[0].wait()
     count = count_ref[0]
     hit, weight, col_t = fill_wanted(cols_ref, count, wanted, slots, blk)
-    seed_load.wait()
+    seed_load(0).wait()
     for b in range(blk):
         nodes = slice(b * TILE, (b + 1) * TILE)
         whole[me * blk + b] = seeds_ref[:rows, nodes].astype(jnp.bfloat16)
@@ -190,6 +217,7 @@
     own_copy.start()
     small[2].wait()
     for h in range(1, halves):
+        seed_load(h).wait()
         for b in range(blk):
             current[h, b] = seeds_ref[
                 h * rows:(h + 1) * rows, b * TILE:(b + 1) * TILE
@@ -208,7 +236,8 @@
             turned[c * per + i] = jnp.transpose(tiles[c * per + i])
         return carry
 
-    lax.fori_loop(0, chunks, turn, 0)
+    early = chunks * 8 // 8
+    lax.fori_loop(0, early, turn, 0)
     for n, peer in enumerate(peers):
         ask(n, peer, peer).wait_recv()
     want_copy.wait()
@@ -232,6 +261,7 @@
 
     for h in range(1, halves):
         exchange(0, h)
+    lax.fori_loop(early, chunks, turn, 0)
     for part in range(PARTS):
         for d in range(1, groups):
             source = origin(d, cores - 1 - core)
@@ -338,9 +368,7 @@
     halves = HALVES if seed_count % (16 * HALVES) == 0 else 1
     rows = seed_count // halves
     peers = panels - 1
-    far = max(panels // (2 if panels % 2 == 0 else 1) - 1, 1)
     vmem = pl.BlockSpec(memory_space=pltpu.VMEM)
-    dma = pltpu.SemaphoreType.DMA
     return pl.pallas_call(
         functools.partial(kernel, panels, slots, blk, seed_count, chunks, unroll, halves),
         out_shape=jax.ShapeDtypeStruct(seeds.shape, jnp.float32),
@@ -361,11 +389,6 @@
             pltpu.VMEM((1, seed_count), jnp.float32),
             pltpu.SMEM((8, square), jnp.int32),
             pltpu.SMEM((panels, 8, width), jnp.int32),
-            dma((chunks,)), dma((1,)), dma((3,)), dma((2,)), dma((peers,)), dma((panels,)),
-            dma((ITERS, halves, peers)), dma((ITERS, halves, panels)),
-            dma((peers,)), dma((panels,)),
-            dma((far, PARTS)), dma((far, PARTS)), dma((far, PARTS)), dma((far, PARTS)),
-            dma((1,)), dma((1,)),
             pltpu.VMEM((panels * blk, rows, TILE), jnp.bfloat16),
             *[
                 pltpu.VMEM((panels * NEED, rows, TILE), jnp.bfloat16)

time: 25.3 us -> 24.6 us (0.972)
  Pallas kernels: 23.7 us -> 22.9 us
    pallas_call x1, Pallas kernels: 23.7 us -> 22.9 us  [per_device(): pl.pallas_call(functools.partial(kernel, panels, slots, blk, seed_count,...]
where the time goes in v3:
time: 24.6 us; the launch traced here: 24.4 us
  Pallas kernels  22.9 us (93%)
  local copies, waits for them, and re-layouts  0.8 us (3%)
  between operations  0.66 us (3%)
    pallas_call x1, Pallas kernels, per_device(): pl.pallas_call(functools.partial(kernel, panels, slots, blk, seed_count,...  22.9 us
    unnamed x1, local copies, waits for them, and re-layouts  0.8 us

profile of v3, /device:TPU:0, one launch (start us, length us, event | category | flops | bytes accessed | tf_op | source)
XLA Modules:
  0.0 24.4 jit_solution(6738647941969246220)
XLA Ops:
  0.7 22.9 %shard_map.64 = f32[32,4096]{1,0:T(8,128)S(1)} custom-call(s32[1]{0:T(128)S(6)} %copy.8.count_ref, s32[1,64]{1,0:T(1,128)} %bitcast.3, s32[1,64]{1,0:T(1,128)} %bitcast.4, f32[1,32]{1,0:T(1,128)} %bitcast.5, f32[32,4096]{1,0:T(8,128)} %seeds_hbm.1, bf16[64,256,256]{2,1,0:T(8,128)(2,1)} %tiles_hbm.1), custom_call_target="tpu_custom_call" | custom-call | tf_op jit(solution)/shard_map/pallas_call | solution.py:372
  23.6 0.8 %copy.9 = f32[32,4096]{1,0:T(8,128)} copy(f32[32,4096]{1,0:T(8,128)S(1)} %shard_map.64) | data formatting | bytes 1048576

commit v4 on v3

--- a/solution.py
+++ b/solution.py
@@ -11,9 +11,11 @@
 NEED = 4
 HALVES = 2
 PARTS = 2
+TAIL = 8
 ITERS = 3
 MESH = pl.DeviceIdType.MESH
 LANES = 128
+CUTS = TILE // LANES
 ROW_PERM, ROW_PLACE, ROW_KEEP, ROW_LAST, ROW_HAS, ROW_COL = 0, 1, 2, 3, 4, 5
 
 
@@ -84,7 +86,7 @@
 
 
 def kernel(
-    panels, slots, blk, seed_count, chunks, unroll, halves,
+    panels, slots, blk, seed_count, chunks, halves,
     count_ref, cols_hbm, rows_hbm, decay_hbm, seeds_hbm, tiles_hbm,
     out_ref,
     tiles, turned, seeds_ref, current, outgoing, partial, own_table, wanted, squares,
@@ -95,20 +97,20 @@
     peers, far = panels - 1, max(panels // (2 if panels % 2 == 0 else 1) - 1, 1)
     pl.run_scoped(
         functools.partial(
-            body, panels, slots, blk, seed_count, chunks, unroll, halves,
+            body, panels, slots, blk, seed_count, chunks, halves,
             count_ref, cols_hbm, rows_hbm, decay_hbm, seeds_hbm, tiles_hbm,
             out_ref,
             tiles, turned, seeds_ref, current, outgoing, partial, own_table, wanted, squares,
             rows_ref, cols_ref, decay_ref, own_s, wanted_s, whole, arrivals,
         ),
         dma((chunks,)), dma((halves,)), dma((3,)), dma((2,)), dma((peers,)), dma((panels,)),
-        dma((ITERS, halves, peers)), dma((ITERS, halves, panels)), dma((peers,)), dma((panels,)),
+        dma((ITERS, halves, CUTS, peers)), dma((ITERS, halves, CUTS, panels)), dma((peers,)), dma((panels,)),
         dma((far, PARTS)), dma((far, PARTS)), dma((far, PARTS)), dma((far, PARTS)), dma((1,)), dma((1,)),
     )
 
 
 def body(
-    panels, slots, blk, seed_count, chunks, unroll, halves,
+    panels, slots, blk, seed_count, chunks, halves,
     count_ref, cols_hbm, rows_hbm, decay_hbm, seeds_hbm, tiles_hbm,
     out_ref,
     tiles, turned, seeds_ref, current, outgoing, partial, own_table, wanted, squares,
@@ -126,6 +128,7 @@
         lax.rem(chip + d, groups) * cores + e
         for d in range(groups - 1, 0, -1) for e in range(cores)
     ] + [chip * cores + lax.rem(core + e, cores) for e in range(1, cores)]
+    away = (groups - 1) * cores
 
     small = [
         pltpu.make_async_copy(src, dst, small_sem.at[n])
@@ -219,9 +222,10 @@
     for h in range(1, halves):
         seed_load(h).wait()
         for b in range(blk):
-            current[h, b] = seeds_ref[
-                h * rows:(h + 1) * rows, b * TILE:(b + 1) * TILE
-            ].astype(jnp.bfloat16)
+            for k in range(CUTS):
+                current[h, k, b] = seeds_ref[
+                    h * rows:(h + 1) * rows, b * TILE + k * LANES:b * TILE + (k + 1) * LANES
+                ].astype(jnp.bfloat16)
     diagonal = lax.broadcasted_iota(jnp.int32, (seed_count, seed_count), 0) == (
         lax.broadcasted_iota(jnp.int32, (seed_count, seed_count), 1)
     )
@@ -242,25 +246,32 @@
         ask(n, peer, peer).wait_recv()
     want_copy.wait()
 
-    def ship(it, h, n, peer, source):
-        return pltpu.make_async_remote_copy(
-            src_ref=outgoing.at[it, h, n],
-            dst_ref=arrivals[it * halves + h].at[pl.ds(source * NEED, NEED)],
-            send_sem=send_sem.at[it, h, n], recv_sem=recv_sem.at[it, h, source],
+    def ship(it, h, k, n, peer, source):
+        return pltpu.make_async_remote_copy(
+            src_ref=outgoing.at[it, h, k, n],
+            dst_ref=arrivals[(it * halves + h) * CUTS + k].at[pl.ds(source * NEED, NEED)],
+            send_sem=send_sem.at[it, h, k, n], recv_sem=recv_sem.at[it, h, k, source],
             device_id={"row": peer}, device_id_type=MESH,
         )
 
-    def exchange(it, h):
-        arrived = arrivals[it * halves + h]
-        for n, peer in enumerate(peers):
-            for k in range(NEED):
-                outgoing[it, h, n, k] = current[h, wanted_s[peer, k, me * blk + blk - 1]]
-            ship(it, h, n, peer, me).start()
-        for k in range(NEED):
-            arrived[me * NEED + k] = current[h, wanted_s[me, k, me * blk + blk - 1]]
+    def exchange(it, h, k):
+        arrived = arrivals[(it * halves + h) * CUTS + k]
+        last = k == CUTS - 1
+        for n, peer in enumerate(peers[:away]):
+            for w in range(NEED):
+                outgoing[it, h, k, n, w] = current[h, k, wanted_s[peer, w, me * blk + blk - 1]]
+            ship(it, h, k, n, peer, me).start()
+        for c in range(CUTS) if last else ():
+            for n, peer in list(enumerate(peers))[away:]:
+                for w in range(NEED):
+                    outgoing[it, h, c, n, w] = current[h, c, wanted_s[peer, w, me * blk + blk - 1]]
+                ship(it, h, c, n, peer, me).start()
+        for w in range(NEED):
+            arrived[me * NEED + w] = current[h, k, wanted_s[me, w, me * blk + blk - 1]]
 
     for h in range(1, halves):
-        exchange(0, h)
+        for k in range(CUTS):
+            exchange(0, h, k)
     lax.fori_loop(early, chunks, turn, 0)
     for part in range(PARTS):
         for d in range(1, groups):
@@ -275,43 +286,60 @@
     for it in range(ITERS):
         for h in range(halves):
             first = it == 0 and h == 0
-            arrived = whole if first else arrivals[it * halves + h]
-            row_at = ROW_COL if first else ROW_PLACE
-            if first and cores > 1:
-                near(partner).wait_recv()
-                for part in range(PARTS):
-                    for d in range(1, groups):
-                        hand(d, part, origin(d, core)).wait_recv()
-            if not first:
-                for n, peer in enumerate(peers):
-                    ship(it, h, n, peer, peer).wait_recv()
-
-            def some(group, acc):
-                for u in range(unroll):
-                    j = group * unroll + u
+            def contract(arrived, place, k, nodes, some, acc):
+                for j in some:
                     product = jnp.dot(
-                        arrived[own_s[row_at, j]], turned[own_s[ROW_PERM, j]],
+                        arrived[own_s[place, j]],
+                        turned[own_s[ROW_PERM, j], nodes, :],
                         preferred_element_type=jnp.float32,
                     )
                     acc = acc * own_s[ROW_KEEP, j].astype(jnp.float32) + product
-                    partial[h, j] = acc
+                    partial[h, k, j] = acc
                 return acc
 
-            lax.fori_loop(0, slots // unroll, some, jnp.zeros((rows, TILE), jnp.float32))
+            zero = jnp.zeros((rows, TILE), jnp.float32)
+            if first:
+                if cores > 1:
+                    near(partner).wait_recv()
+                    for part in range(PARTS):
+                        for d in range(1, groups):
+                            hand(d, part, origin(d, core)).wait_recv()
+                contract(whole, ROW_COL, 0, slice(0, TILE), range(slots), zero)
+            else:
+                rest = range(0)
+                for k in range(CUTS):
+                    for n, peer in enumerate(peers):
+                        ship(it, h, k, n, peer, peer).wait_recv()
+                    if k > 0:
+                        contract(*use, rest, acc)
+                    use = (
+                        arrivals[(it * halves + h) * CUTS + k], ROW_PLACE, k,
+                        slice(k * LANES, (k + 1) * LANES),
+                    )
+                    cut = slots - TAIL if k < CUTS - 1 else slots
+                    acc = contract(*use, range(cut), zero)
+                    rest = range(cut, slots)
 
             mine = slice(h * rows, (h + 1) * rows)
-            total = jnp.zeros((rows, TILE), jnp.float32)
-            for r in range(blk):
-                summed = partial[h, own_s[ROW_LAST, r]] * own_s[ROW_HAS, r].astype(jnp.float32)
-                value = decay[mine] * summed + seeds_ref[mine, r * TILE:(r + 1) * TILE]
+            total = jnp.zeros((rows, LANES), jnp.float32)
+            for k in range(CUTS):
+                out = slice(k * LANES, (k + 1) * LANES)
+                for r in range(blk):
+                    last = own_s[ROW_LAST, r]
+                    summed = partial[h, 0, last, :, out]
+                    for c in range(1, 1 if first else CUTS):
+                        summed = summed + partial[h, c, last, :, out]
+                    summed = summed * own_s[ROW_HAS, r].astype(jnp.float32)
+                    nodes = slice(r * TILE + k * LANES, r * TILE + (k + 1) * LANES)
+                    value = decay[mine] * summed + seeds_ref[mine, nodes]
+                    if it < ITERS - 1:
+                        current[h, k, r] = value.astype(jnp.bfloat16)
+                    else:
+                        out_ref[mine, nodes] = value
+                        total = total + value * value
                 if it < ITERS - 1:
-                    current[h, r] = value.astype(jnp.bfloat16)
-                else:
-                    out_ref[mine, r * TILE:(r + 1) * TILE] = value
-                    total = total + value * value
-            if it < ITERS - 1:
-                exchange(it + 1, h)
-            else:
+                    exchange(it + 1, h, k)
+            if it == ITERS - 1:
                 totals.append(jnp.sum(total, axis=1, keepdims=True))
 
     lane = lax.broadcasted_iota(jnp.int32, (8, LANES), 1)
@@ -333,8 +361,9 @@
     for n, peer in enumerate(peers):
         for it in range(ITERS):
             for h in range(halves):
-                if (it, h) != (0, 0):
-                    ship(it, h, n, peer, me).wait_send()
+                for k in range(CUTS):
+                    if (it, h) != (0, 0):
+                        ship(it, h, k, n, peer, me).wait_send()
         ask(n, peer, me).wait_send()
     for part in range(PARTS):
         for d in range(1, groups):
@@ -364,13 +393,12 @@
     width = -(-panels * blk // LANES) * LANES
     square = max(LANES, slots)
     chunks = 8 if slots % 8 == 0 else 1
-    unroll = 64 if slots % 64 == 0 else 1
     halves = HALVES if seed_count % (16 * HALVES) == 0 else 1
     rows = seed_count // halves
     peers = panels - 1
     vmem = pl.BlockSpec(memory_space=pltpu.VMEM)
     return pl.pallas_call(
-        functools.partial(kernel, panels, slots, blk, seed_count, chunks, unroll, halves),
+        functools.partial(kernel, panels, slots, blk, seed_count, chunks, halves),
         out_shape=jax.ShapeDtypeStruct(seeds.shape, jnp.float32),
         in_specs=[pl.BlockSpec(memory_space=pltpu.SMEM)] + [pl.BlockSpec(memory_space=pltpu.HBM)] * 5,
         out_specs=vmem,
@@ -378,9 +406,9 @@
             pltpu.VMEM((slots, TILE, TILE), jnp.bfloat16),
             pltpu.VMEM((slots, TILE, TILE), jnp.bfloat16),
             pltpu.VMEM(seeds.shape, jnp.float32),
-            pltpu.VMEM((halves, blk, rows, TILE), jnp.bfloat16),
-            pltpu.VMEM((ITERS, halves, peers, NEED, rows, TILE), jnp.bfloat16),
-            pltpu.VMEM((halves, slots, rows, TILE), jnp.float32),
+            pltpu.VMEM((halves, CUTS, blk, rows, LANES), jnp.bfloat16),
+            pltpu.VMEM((ITERS, halves, CUTS, peers, NEED, rows, LANES), jnp.bfloat16),
+            pltpu.VMEM((halves, CUTS, slots, rows, TILE), jnp.float32),
             pltpu.VMEM((8, square), jnp.int32),
             pltpu.VMEM((8, width), jnp.int32),
             pltpu.VMEM((panels, 8, LANES), jnp.float32),
@@ -391,8 +419,8 @@
             pltpu.SMEM((panels, 8, width), jnp.int32),
             pltpu.VMEM((panels * blk, rows, TILE), jnp.bfloat16),
             *[
-                pltpu.VMEM((panels * NEED, rows, TILE), jnp.bfloat16)
-                for _ in range(ITERS * halves)
+                pltpu.VMEM((panels * NEED, rows, LANES), jnp.bfloat16)
+                for _ in range(ITERS * halves * CUTS)
             ],
         ],
         compiler_params=pltpu.CompilerParams(

time: 24.6 us -> 24.2 us (0.984)
  Pallas kernels: 22.9 us -> 22.5 us
    pallas_call x1, Pallas kernels: 22.9 us -> 22.5 us  [per_device(): pl.pallas_call(functools.partial(kernel, panels, slots, blk, seed_count,...]
where the time goes in v4:
time: 24.2 us; the launch traced here: 24 us
  Pallas kernels  22.5 us (93%)
  local copies, waits for them, and re-layouts  0.8 us (3%)
  between operations  0.66 us (3%)
    pallas_call x1, Pallas kernels, per_device(): pl.pallas_call(functools.partial(kernel, panels, slots, blk, seed_count,...  22.5 us
    unnamed x1, local copies, waits for them, and re-layouts  0.8 us

profile of v4, /device:TPU:0, one launch (start us, length us, event | category | flops | bytes accessed | tf_op | source)
XLA Modules:
  0.0 24.0 jit_solution(15463399332348383751)
XLA Ops:
  0.7 22.5 %shard_map.64 = f32[32,4096]{1,0:T(8,128)S(1)} custom-call(s32[1]{0:T(128)S(6)} %copy.8.count_ref, s32[1,64]{1,0:T(1,128)} %bitcast.3, s32[1,64]{1,0:T(1,128)} %bitcast.4, f32[1,32]{1,0:T(1,128)} %bitcast.5, f32[32,4096]{1,0:T(8,128)} %seeds_hbm.1, bf16[64,256,256]{2,1,0:T(8,128)(2,1)} %tiles_hbm.1), custom_call_target="tpu_custom_call" | custom-call | tf_op jit(solution)/shard_map/pallas_call | solution.py:400
  23.2 0.8 %copy.9 = f32[32,4096]{1,0:T(8,128)} copy(f32[32,4096]{1,0:T(8,128)S(1)} %shard_map.64) | data formatting | bytes 1048576

commit v5 on v4

--- a/solution.py
+++ b/solution.py
@@ -10,7 +10,6 @@
 TILE = 256
 NEED = 4
 HALVES = 2
-PARTS = 2
 TAIL = 8
 ITERS = 3
 MESH = pl.DeviceIdType.MESH
@@ -91,8 +90,9 @@
     out_ref,
     tiles, turned, seeds_ref, current, outgoing, partial, own_table, wanted, squares,
     rows_ref, cols_ref, decay_ref, own_s, wanted_s,
-    whole, *arrivals,
+    *landing,
 ):
+    whole, arrivals = landing[:CUTS], landing[CUTS:]
     dma = pltpu.SemaphoreType.DMA
     peers, far = panels - 1, max(panels // (2 if panels % 2 == 0 else 1) - 1, 1)
     pl.run_scoped(
@@ -105,7 +105,7 @@
         ),
         dma((chunks,)), dma((halves,)), dma((3,)), dma((2,)), dma((peers,)), dma((panels,)),
         dma((ITERS, halves, CUTS, peers)), dma((ITERS, halves, CUTS, panels)), dma((peers,)), dma((panels,)),
-        dma((far, PARTS)), dma((far, PARTS)), dma((far, PARTS)), dma((far, PARTS)), dma((1,)), dma((1,)),
+        dma((far, CUTS)), dma((far, CUTS)), dma((far, CUTS)), dma((far, CUTS)), dma((CUTS,)), dma((CUTS,)),
     )
 
 
@@ -163,24 +163,24 @@
     hit, weight, col_t = fill_wanted(cols_ref, count, wanted, slots, blk)
     seed_load(0).wait()
     for b in range(blk):
-        nodes = slice(b * TILE, (b + 1) * TILE)
-        whole[me * blk + b] = seeds_ref[:rows, nodes].astype(jnp.bfloat16)
+        for k in range(CUTS):
+            nodes = slice(b * TILE + k * LANES, b * TILE + (k + 1) * LANES)
+            whole[k][me * blk + b] = seeds_ref[:rows, nodes].astype(jnp.bfloat16)
     pl.semaphore_wait(barrier, panels - 1)
 
     def ask(n, peer, source):
         return pltpu.make_async_remote_copy(
-            src_ref=wanted, dst_ref=wanted_s.at[source],
+            src_ref=wanted.at[pl.ds(0, NEED)], dst_ref=wanted_s.at[source, pl.ds(0, NEED)],
             send_sem=want_send.at[n], recv_sem=want_recv.at[source],
             device_id={"row": peer}, device_id_type=MESH,
         )
 
     for n, peer in enumerate(peers):
         ask(n, peer, me).start()
-    span = blk // PARTS
     partner = chip * cores + (cores - 1 - core)
 
     def block(source, part):
-        return whole.at[pl.ds(source * blk + part * span, span)]
+        return whole[part].at[pl.ds(source * blk, blk)]
 
     def bulk(d, part, source):
         far = lax.rem(chip + d, groups) * cores + (cores - 1 - core)
@@ -197,21 +197,22 @@
             device_id={"row": partner}, device_id_type=MESH,
         )
 
-    def near(source):
-        return pltpu.make_async_remote_copy(
-            src_ref=whole.at[pl.ds(source * blk, blk)], dst_ref=whole.at[pl.ds(source * blk, blk)],
-            send_sem=near_send.at[0], recv_sem=near_recv.at[0],
+    def near(part, source):
+        return pltpu.make_async_remote_copy(
+            src_ref=block(source, part), dst_ref=block(source, part),
+            send_sem=near_send.at[part], recv_sem=near_recv.at[part],
             device_id={"row": partner}, device_id_type=MESH,
         )
 
     def origin(d, index):
         return lax.rem(chip + groups - d, groups) * cores + index
 
-    for part in range(PARTS):
+    for part in range(CUTS):
         for d in range(1, groups):
             bulk(d, part, me).start()
     if cores > 1:
-        near(me).start()
+        for part in range(CUTS):
+            near(part, me).start()
     want_copy = pltpu.make_async_copy(wanted, wanted_s.at[me], table_sem.at[1])
     want_copy.start()
     small[1].wait()
@@ -273,7 +274,7 @@
         for k in range(CUTS):
             exchange(0, h, k)
     lax.fori_loop(early, chunks, turn, 0)
-    for part in range(PARTS):
+    for part in range(CUTS):
         for d in range(1, groups):
             source = origin(d, cores - 1 - core)
             bulk(d, part, source).wait_recv()
@@ -298,27 +299,27 @@
                 return acc
 
             zero = jnp.zeros((rows, TILE), jnp.float32)
-            if first:
-                if cores > 1:
-                    near(partner).wait_recv()
-                    for part in range(PARTS):
-                        for d in range(1, groups):
-                            hand(d, part, origin(d, core)).wait_recv()
-                contract(whole, ROW_COL, 0, slice(0, TILE), range(slots), zero)
-            else:
-                rest = range(0)
-                for k in range(CUTS):
+            def arrive(k):
+                if not first:
                     for n, peer in enumerate(peers):
                         ship(it, h, k, n, peer, peer).wait_recv()
-                    if k > 0:
-                        contract(*use, rest, acc)
-                    use = (
-                        arrivals[(it * halves + h) * CUTS + k], ROW_PLACE, k,
-                        slice(k * LANES, (k + 1) * LANES),
-                    )
-                    cut = slots - TAIL if k < CUTS - 1 else slots
-                    acc = contract(*use, range(cut), zero)
-                    rest = range(cut, slots)
+                elif cores > 1:
+                    near(k, partner).wait_recv()
+                    for d in range(1, groups):
+                        hand(d, k, origin(d, core)).wait_recv()
+
+            rest = range(0)
+            for k in range(CUTS):
+                arrive(k)
+                if k > 0:
+                    contract(*use, rest, acc)
+                use = (
+                    whole[k] if first else arrivals[(it * halves + h) * CUTS + k],
+                    ROW_COL if first else ROW_PLACE, k, slice(k * LANES, (k + 1) * LANES),
+                )
+                cut = slots - TAIL if k < CUTS - 1 else slots
+                acc = contract(*use, range(cut), zero)
+                rest = range(cut, slots)
 
             mine = slice(h * rows, (h + 1) * rows)
             total = jnp.zeros((rows, LANES), jnp.float32)
@@ -327,7 +328,7 @@
                 for r in range(blk):
                     last = own_s[ROW_LAST, r]
                     summed = partial[h, 0, last, :, out]
-                    for c in range(1, 1 if first else CUTS):
+                    for c in range(1, CUTS):
                         summed = summed + partial[h, c, last, :, out]
                     summed = summed * own_s[ROW_HAS, r].astype(jnp.float32)
                     nodes = slice(r * TILE + k * LANES, r * TILE + (k + 1) * LANES)
@@ -365,13 +366,14 @@
                     if (it, h) != (0, 0):
                         ship(it, h, k, n, peer, me).wait_send()
         ask(n, peer, me).wait_send()
-    for part in range(PARTS):
+    for part in range(CUTS):
         for d in range(1, groups):
             bulk(d, part, me).wait_send()
             if cores > 1:
                 hand(d, part, origin(d, cores - 1 - core)).wait_send()
     if cores > 1:
-        near(me).wait_send()
+        for part in range(CUTS):
+            near(part, me).wait_send()
     for n, peer in enumerate(peers):
         share(n, peer, peer).wait_recv()
     every = squares[0]
@@ -417,7 +419,7 @@
             pltpu.VMEM((1, seed_count), jnp.float32),
             pltpu.SMEM((8, square), jnp.int32),
             pltpu.SMEM((panels, 8, width), jnp.int32),
-            pltpu.VMEM((panels * blk, rows, TILE), jnp.bfloat16),
+            *[pltpu.VMEM((panels * blk, rows, LANES), jnp.bfloat16) for _ in range(CUTS)],
             *[
                 pltpu.VMEM((panels * NEED, rows, LANES), jnp.bfloat16)
                 for _ in range(ITERS * halves * CUTS)

time: 24.2 us -> 23.6 us (0.975)
  Pallas kernels: 22.5 us -> 22 us
    pallas_call x1, Pallas kernels: 22.5 us -> 22 us  [per_device(): pl.pallas_call(functools.partial(kernel, panels, slots, blk, seed_count,...]
where the time goes in v5:
time: 23.6 us; the launch traced here: 23.4 us
  Pallas kernels  22 us (93%)
  local copies, waits for them, and re-layouts  0.8 us (3%)
  between operations  0.66 us (3%)
    pallas_call x1, Pallas kernels, per_device(): pl.pallas_call(functools.partial(kernel, panels, slots, blk, seed_count,...  22 us
    unnamed x1, local copies, waits for them, and re-layouts  0.8 us

profile of v5, /device:TPU:0, one launch (start us, length us, event | category | flops | bytes accessed | tf_op | source)
XLA Modules:
  0.0 23.4 jit_solution(1892321410557981255)
XLA Ops:
  0.7 22.0 %shard_map.64 = f32[32,4096]{1,0:T(8,128)S(1)} custom-call(s32[1]{0:T(128)S(6)} %copy.8.count_ref, s32[1,64]{1,0:T(1,128)} %bitcast.3, s32[1,64]{1,0:T(1,128)} %bitcast.4, f32[1,32]{1,0:T(1,128)} %bitcast.5, f32[32,4096]{1,0:T(8,128)} %seeds_hbm.1, bf16[64,256,256]{2,1,0:T(8,128)(2,1)} %tiles_hbm.1), custom_call_target="tpu_custom_call" | custom-call | tf_op jit(solution)/shard_map/pallas_call | solution.py:402
  22.6 0.8 %copy.9 = f32[32,4096]{1,0:T(8,128)} copy(f32[32,4096]{1,0:T(8,128)S(1)} %shard_map.64) | data formatting | bytes 1048576

commit v6 on v5

--- a/solution.py
+++ b/solution.py
@@ -162,10 +162,12 @@
     count = count_ref[0]
     hit, weight, col_t = fill_wanted(cols_ref, count, wanted, slots, blk)
     seed_load(0).wait()
-    for b in range(blk):
-        for k in range(CUTS):
+    def convert(k):
+        for b in range(blk):
             nodes = slice(b * TILE + k * LANES, b * TILE + (k + 1) * LANES)
             whole[k][me * blk + b] = seeds_ref[:rows, nodes].astype(jnp.bfloat16)
+
+    convert(0)
     pl.semaphore_wait(barrier, panels - 1)
 
     def ask(n, peer, source):
@@ -208,6 +210,8 @@
         return lax.rem(chip + groups - d, groups) * cores + index
 
     for part in range(CUTS):
+        if part > 0:
+            convert(part)
         for d in range(1, groups):
             bulk(d, part, me).start()
     if cores > 1:
@@ -379,7 +383,7 @@
     every = squares[0]
     for p in range(1, panels):
         every = every + squares[p]
-    scale = 1.0 / jnp.sqrt(every / (panels * blk * TILE) + 1e-06)
+    scale = lax.rsqrt(every / (panels * blk * TILE) + 1e-06)
     for i in range(len(pieces)):
         one = jnp.sum(jnp.where(lane == i, scale, 0.0), axis=1, keepdims=True)
         out_ref[i * 8:(i + 1) * 8, :] = out_ref[i * 8:(i + 1) * 8, :] * one

time: 23.6 us -> 23.6 us (level)
  no operation moved by 1% of the time
where the time goes in v6:
time: 23.6 us; the launch traced here: 23.4 us
  Pallas kernels  22 us (93%)
  local copies, waits for them, and re-layouts  0.8 us (3%)
  between operations  0.66 us (3%)
    pallas_call x1, Pallas kernels, per_device(): pl.pallas_call(functools.partial(kernel, panels, slots, blk, seed_count,...  22 us
    unnamed x1, local copies, waits for them, and re-layouts  0.8 us

profile of v6, /device:TPU:0, one launch (start us, length us, event | category | flops | bytes accessed | tf_op | source)
XLA Modules:
  0.0 23.4 jit_solution(10150654572966224338)
XLA Ops:
  0.7 22.0 %shard_map.64 = f32[32,4096]{1,0:T(8,128)S(1)} custom-call(s32[1]{0:T(128)S(6)} %copy.8.count_ref, s32[1,64]{1,0:T(1,128)} %bitcast.3, s32[1,64]{1,0:T(1,128)} %bitcast.4, f32[1,32]{1,0:T(1,128)} %bitcast.5, f32[32,4096]{1,0:T(8,128)} %seeds_hbm.1, bf16[64,256,256]{2,1,0:T(8,128)(2,1)} %tiles_hbm.1), custom_call_target="tpu_custom_call" | custom-call | tf_op jit(solution)/shard_map/pallas_call | solution.py:406
  22.6 0.8 %copy.9 = f32[32,4096]{1,0:T(8,128)} copy(f32[32,4096]{1,0:T(8,128)S(1)} %shard_map.64) | data formatting | bytes 1048576
